TPU v7x, 256 devices: a whole 4x4x8 slice. The times are simulated.
256 devices in a mesh: nodes: 64 (over z, x, core), heads: 4 (over y).
Axes of the slice: x: 4, y: 4, z: 8, core: 2. Of those that a mesh axis runs over, the one named last changes fastest.
Arguments:
- nodes_in: bfloat16 [32768, 1024], P('nodes', 'heads'), may hold values from -6 to 6
- local_gain: float32 [1024], replicated, may hold values from 0.5 to 1.5
- neighbour_query_key_value: bfloat16 [3, 1024, 1024], P(None, None, 'heads'), may hold values from -0.25 to 0.25
- local_out: bfloat16 [1024, 1024], P('heads'), may hold values from -0.1875 to 0.1875
- global_gain: float32 [1024], replicated, may hold values from 0.5 to 1.5
- global_qkv: bfloat16 [3, 1024, 1024], P(None, None, 'heads'), may hold values from -0.1875 to 0.1875
- global_out: bfloat16 [1024, 1024], P('heads'), may hold values from -1.875 to 1.875
- feature_map: bfloat16 [16, 64, 128], P('heads'), may hold values from -5 to 5
- neighbour_count: int32 [256], P('nodes'), may hold values from 1 to 8
- neighbour_blocks: int32 [256, 8], P('nodes'), may hold values from 0 to 255, as said below
- metis_order: int32 [256], P('nodes'), may hold values from 0 to 255, as said below
- hashed_order: int32 [256], P('nodes'), may hold values from 0 to 255, as said below
Outputs:
- output: bfloat16 [32768, 1024], P('nodes', 'heads')
Inputs may be any that keep to these rules, and one draw needn't show every extreme that they name: `neighbour_blocks`: entry 0 of block b's list is b itself; every entry lies within 2 blocks of the aligned group of 4 blocks that holds b, inside the graph; entries from neighbour_count on are unused; entries may repeat. `metis_order`: A permutation of the block ids. `hashed_order`: A permutation of the block ids. The blocks at the 4 METIS positions of aligned group g go to the aligned groups of 4 hashed positions numbered (g + k * 16) modulo 64 for k = 0 to 3, exactly 1 of them to each; which block goes to which of these groups, and to which position in it, is drawn.
All inputs are finite; a program needn't handle non-finite values.
Results may differ from a plain program's by a relative error of at most 0.015.
Values may be sent and summed in bfloat16 or wider, within the bound.
No kernel may reach another device: no remote copies, remote signals or barrier semaphores. Data moves between devices by JAX's collectives and lax.ppermute only.
A program may use at most 64 MiB of HBM per device.

v0:
```python
import jax
import jax.numpy as jnp
from jax import lax
from jax.sharding import PartitionSpec as P

HD = 64
BLOCK = 128
HALO_BLK = 2
EPSILON = 1e-06


def passed_along(value, axis, steps):
    count = lax.axis_size(axis)
    pairs = [(source, (source + steps) % count) for source in range(count)]
    return lax.ppermute(value, axis, pairs)


def gathered_total(array, axis):
    parts = lax.all_gather(array, axis)
    return parts.sum(axis=0)


def laid_out(parts, dim):
    parts = jnp.moveaxis(parts, 0, dim)
    dims = parts.shape
    return parts.reshape(*dims[:dim], dims[dim] * dims[dim + 1], *dims[dim + 2 :])


def copy_for_each(array, axis):
    copies = jnp.broadcast_to(array, (lax.axis_size(axis), *array.shape))
    return lax.all_to_all(copies, axis, split_axis=0, concat_axis=0, tiled=True)


def collect(array, axis, dim):
    return laid_out(copy_for_each(array, axis), dim)


def padded(array, sides, width):
    for axis, dim in sides:
        count, length = (lax.axis_size(axis), array.shape[dim])
        up = [(i, (i + 1) % count) for i in range(count - 1)]
        down = [(j, i) for i, j in up]
        last = lax.slice_in_dim(array, length - width, length, axis=dim)
        initial = lax.slice_in_dim(array, 0, width, axis=dim)
        before = lax.ppermute(last, axis, up)
        after = lax.ppermute(initial, axis, down)
        array = jnp.concatenate([before, array, after], axis=dim)
    return array


def cut_along(array, dim, count):
    dims = array.shape
    parts = array.reshape(*dims[:dim], count, dims[dim] // count, *dims[dim + 1 :])
    return jnp.moveaxis(parts, dim, 0)


def summed_on_arrival(array, axis, dim):
    count = lax.axis_size(axis)
    parts = lax.all_to_all(cut_along(array, dim, count), axis, 0, 0, tiled=True)
    return jnp.sum(parts.astype(jnp.float32), axis=0)


def root_scale(row_data, gain_vector):
    as_float = row_data.astype(jnp.float32)
    mean_square = jnp.mean(as_float * as_float, axis=-1, keepdims=True)
    return (as_float * lax.rsqrt(mean_square + EPSILON) * gain_vector).astype(jnp.bfloat16)


def local_attention(queries, extended, counts, local_index):
    block_count = counts.shape[0]
    list_slots = local_index.shape[1]
    group_size = 4
    feature_width = queries.shape[1]
    heads_local = feature_width // HD
    key_blocks = extended.reshape(2, -1, BLOCK, feature_width)
    query_groups = queries.reshape(block_count // group_size, group_size, BLOCK, heads_local, HD)
    slot_of_key = jnp.arange(list_slots * BLOCK, dtype=jnp.int32) // BLOCK

    def one_group(inputs):
        query_group, index_group, count_group = inputs
        picked = key_blocks[:, index_group].reshape(
            2, group_size, list_slots * BLOCK, heads_local, HD
        )
        scores = jnp.einsum(
            "gqhd,gkhd->ghqk", query_group, picked[0], preferred_element_type=jnp.float32
        ) * HD ** (-0.5)
        live = slot_of_key[None, :] < count_group[:, None]
        scores = jnp.where(live[:, None, None, :], scores, -jnp.inf)
        row_max = jnp.max(scores, axis=-1, keepdims=True)
        expo = jnp.exp(scores - row_max)
        totals = jnp.sum(expo, axis=-1)
        local_weights = expo.astype(jnp.bfloat16)
        mixed_heads = jnp.einsum(
            "ghqk,gkhd->gqhd", local_weights, picked[1], preferred_element_type=jnp.float32
        )
        mixed_heads = mixed_heads / jnp.transpose(totals, (0, 2, 1))[..., None]
        return mixed_heads.astype(jnp.bfloat16)

    mixed_all = lax.map(
        one_group,
        (
            query_groups,
            local_index.reshape(block_count // group_size, group_size, list_slots),
            counts.reshape(block_count // group_size, group_size),
        ),
    )
    return mixed_all.reshape(block_count * BLOCK, feature_width)


def relayout(row_data, metis_local, all_hashed, device_nodes):
    block_count = metis_local.shape[0]
    devices = lax.axis_size("nodes")
    lane_count = min(block_count, devices)
    stride = max(1, devices // block_count)
    slot_limit = block_count // lane_count
    feature_width = row_data.shape[1]
    total_blocks = all_hashed.shape[0]
    matches = all_hashed[None, :] == metis_local[:, None]
    target = jnp.sum(
        jnp.where(matches, jnp.arange(total_blocks, dtype=jnp.int32)[None, :], 0), axis=1
    )
    steps_away = (target // block_count - device_nodes) % devices // stride
    order_ids = jnp.arange(block_count, dtype=jnp.int32)
    earlier = (steps_away[None, :] == steps_away[:, None]) & (
        order_ids[None, :] < order_ids[:, None]
    )
    rank_within = jnp.sum(earlier.astype(jnp.int32), axis=1)
    lane_id = rank_within * lane_count + steps_away
    chosen = lane_id[None, :] == order_ids[:, None]
    source = jnp.sum(jnp.where(chosen, order_ids[None, :], 0), axis=1)
    lane_target = jnp.sum(jnp.where(chosen, target[None, :], 0), axis=1)
    blocks = row_data.reshape(block_count, BLOCK, feature_width)
    outgoing = blocks[source].reshape(slot_limit, lane_count, BLOCK, feature_width)
    positions = lane_target.reshape(slot_limit, lane_count)
    block_pieces = [outgoing[:, :1]]
    position_pieces = [positions[:, :1]]
    for lane_step in range(1, lane_count):
        arrived, arrived_at = passed_along(
            (outgoing[:, lane_step : lane_step + 1], positions[:, lane_step : lane_step + 1]),
            "nodes",
            lane_step * stride,
        )
        block_pieces.append(arrived)
        position_pieces.append(arrived_at)
    incoming = jnp.concatenate(block_pieces, axis=1)
    in_position = jnp.concatenate(position_pieces, axis=1)
    local_position = in_position.reshape(block_count) - device_nodes * block_count
    located = local_position[None, :] == order_ids[:, None]
    picked_lane = jnp.sum(jnp.where(located, order_ids[None, :], 0), axis=1)
    return incoming.reshape(block_count, BLOCK, feature_width)[picked_lane].reshape(
        block_count * BLOCK, feature_width
    )


def gather_rows(shard_rows):
    return lax.all_gather(shard_rows, "heads", axis=1, tiled=True)


def global_mixing(full_rows, gain_vector, triple_weight, feature_map, out_weight):
    rescaled_input = root_scale(full_rows, gain_vector)
    triple = jnp.einsum(
        "au,nuz->naz", rescaled_input, triple_weight, preferred_element_type=jnp.float32
    ).astype(jnp.bfloat16)
    row_count = full_rows.shape[0]
    heads_local = feature_map.shape[0]

    def feature_maps(head_rows):
        angles = jnp.einsum(
            "nhd,hdf->nhf",
            head_rows.reshape(row_count, heads_local, HD),
            feature_map,
            preferred_element_type=jnp.float32,
        ) * HD ** (-0.5)
        return (jax.nn.elu(angles) + 1.0).astype(jnp.bfloat16)

    phi_query = feature_maps(triple[0])
    phi_key = feature_maps(triple[1])
    head_values = triple[2].reshape(row_count, heads_local, HD)
    summary = jnp.einsum("nhf,nhd->hfd", phi_key, head_values, preferred_element_type=jnp.float32)
    key_total = jnp.sum(phi_key.astype(jnp.float32), axis=0)
    summary, key_total = (gathered_total(summary, "nodes"), gathered_total(key_total, "nodes"))
    query_float = phi_query.astype(jnp.float32)
    numerator = jnp.einsum("nhf,hfd->nhd", query_float, summary, precision=lax.Precision.HIGHEST)
    denominator = jnp.einsum("nhf,hf->nh", query_float, key_total, precision=lax.Precision.HIGHEST)
    global_mixed = (
        (numerator / denominator[..., None])
        .astype(jnp.bfloat16)
        .reshape(row_count, heads_local * HD)
    )
    return jnp.dot(global_mixed, out_weight, preferred_element_type=jnp.float32)


def body(
    nodes_in,
    local_gain,
    neighbour_query_key_value,
    local_out,
    global_gain,
    global_qkv,
    global_out,
    feature_map,
    neighbour_count,
    neighbour_blocks,
    metis_order,
    hashed_order,
):
    block_count = metis_order.shape[0]
    device_nodes = lax.axis_index("nodes")
    all_hashed = collect(hashed_order, "nodes", 0)
    full_input = collect(nodes_in, "heads", 1)
    local_rescaled = root_scale(full_input, local_gain)
    triple = jnp.einsum(
        "au,nuz->naz", local_rescaled, neighbour_query_key_value, preferred_element_type=jnp.float32
    ).astype(jnp.bfloat16)
    rim_rows = HALO_BLK * BLOCK
    extended = padded(triple[1:], (("nodes", 1),), rim_rows)
    first_block = device_nodes * block_count - HALO_BLK
    local_index = neighbour_blocks - first_block
    local_mixed = local_attention(triple[0], extended, neighbour_count, local_index)
    partial_value = jnp.dot(local_mixed, local_out, preferred_element_type=jnp.float32)
    summed = lax.psum_scatter(
        partial_value.astype(jnp.bfloat16), "heads", scatter_dimension=1, tiled=True
    ).astype(jnp.float32)
    hidden = (nodes_in.astype(jnp.float32) + summed).astype(jnp.bfloat16)
    full_rows = gather_rows(hidden)
    global_partial = global_mixing(full_rows, global_gain, global_qkv, feature_map, global_out)
    global_summed = summed_on_arrival(global_partial.astype(jnp.bfloat16), "heads", 1)
    result = (hidden.astype(jnp.float32) + global_summed).astype(jnp.bfloat16)
    result = relayout(result, metis_order, all_hashed, device_nodes)
    return result


def solution(mesh):
    in_specs = (
        P("nodes", "heads"),
        P(),
        P(None, None, "heads"),
        P("heads", None),
        P(),
        P(None, None, "heads"),
        P("heads", None),
        P("heads", None, None),
        P("nodes"),
        P("nodes", None),
        P("nodes"),
        P("nodes"),
    )
    out_specs = P("nodes", "heads")
    return jax.shard_map(body, mesh=mesh, in_specs=in_specs, out_specs=out_specs, check_vma=False)
```

profile of v0, /device:TPU:33, one launch (start us, length us, event | category | flops | bytes accessed | tf_op | source)
XLA Modules:
  0.0 270.1 jit_solution(14255202605277190932)
XLA Ops:
  6.5 2.2 broadcast_in_dim.96
  8.7 4.2 %all-to-all-start = ((bf16[4,512,256]{2,1,0:T(8,128)(2,1)}), bf16[4,512,256]{2,1,0:T(8,128)(2,1)}, u32[]{:S(2)}, u32[]{:S(2)}) async-start(bf16[4,512,256]{2,1,0:T(8,128)(2,1)} %broadcast_in_dim.96), calls=%async_computation | async-start | bytes 2097152 | tf_op jit(solution)/shard_map/all_to_all | solution.py:31
  13.1 14.1 %all-to-all-done = bf16[4,512,256]{2,1,0:T(8,128)(2,1)} async-done(((bf16[4,512,256]{2,1,0:T(8,128)(2,1)}), bf16[4,512,256]{2,1,0:T(8,128)(2,1)}, u32[]{:S(2)}, u32[]{:S(2)}) %all-to-all-start) | async-done | bytes 1048608 | tf_op jit(solution)/shard_map/all_to_all | solution.py:31
  27.3 1.5 copy.35
  29.4 1.0 fusion.13
  30.5 3.7 %collective-permute-start.1 = (bf16[2,256,256]{2,1,0:T(8,128)(2,1)S(1)}, bf16[2,256,256]{2,1,0:T(8,128)(2,1)S(1)}, u32[]{:S(2)}, u32[]{:S(2)}) collective-permute-start(bf16[2,256,256]{2,1,0:T(8,128)(2,1)S(1)} %get-tuple-element.34), channel_id=1, source_target_pairs={{4,0},{8,4},{12,8},{16,12},{20,16},{24,20},{28,24},{32,28},{36,32}... | collective-permute-start | bytes 786440 | tf_op jit(solution)/shard_map/ppermute | solution.py:46
  34.2 3.0 %collective-permute-start = (bf16[2,256,256]{2,1,0:T(8,128)(2,1)S(1)}, bf16[2,256,256]{2,1,0:T(8,128)(2,1)}, u32[]{:S(2)}, u32[]{:S(2)}) collective-permute-start(bf16[2,256,256]{2,1,0:T(8,128)(2,1)S(1)} %get-tuple-element.33), channel_id=1, source_target_pairs={{0,4},{4,8},{8,12},{12,16},{16,20},{20,24},{24,28},{28,32},{32,36}... | collective-permute-start | bytes 786440 | tf_op jit(solution)/shard_map/ppermute | solution.py:45
  37.3 0.8 slice.81
  38.4 0.9 collective-permute-done.1
  39.3 1.2 collective-permute-done
  40.5 1.2 pad_maximum_fusion
  41.7 2.8 %gather_fusion = bf16[32,2,128,256]{3,2,1,0:T(8,128)(2,1)} fusion(bf16[2,8,128,256]{3,2,1,0:T(8,128)(2,1)S(1)} %bitcast.121, s32[1024]{0:T(1024)S(1)} %pad_clamp_fusion.2), kind=kCustom, calls=%fused_computation | custom fusion | bytes 8388736 | tf_op jit(solution)/shard_map/while/body/eval_jaxpr/gather | solution.py:81
  44.5 7.5 %copy.37 = bf16[4,8,2,128,256]{3,1,4,0,2:T(8,128)(2,1)} copy(bf16[4,8,2,128,256]{4,3,2,1,0:T(8,128)(2,1)} %bitcast.122) | data formatting | bytes 8388608 | tf_op jit(solution)/shard_map/while/body/eval_jaxpr/gather | solution.py:81
  52.0 4.5 %fusion.50 = (bf16[1,4,8,128,256]{3,2,4,1,0:T(8,128)(2,1)}, bf16[1,4,8,128,256]{3,2,4,1,0:T(8,128)(2,1)}) fusion(bf16[2,4,8,128,256]{3,2,4,1,0:T(8,128)(2,1)} %bitcast.123), kind=kLoop, calls=%fused_computation.104 | loop fusion | bytes 8388608 | tf_op jit(solution)/shard_map/while/body/eval_jaxpr/slice | solution.py:85
  56.5 4.2 %squeeze.19 = bf16[4,1024,4,64]{1,3,2,0:T(8,128)(2,1)} reshape(bf16[1,4,8,128,256]{3,2,4,1,0:T(8,128)(2,1)} %get-tuple-element.20) | data formatting | bytes 4194304 | tf_op jit(solution)/shard_map/while/body/eval_jaxpr/squeeze | solution.py:94
  60.7 4.2 %squeeze.21 = bf16[4,1024,4,64]{1,3,2,0:T(8,128)(2,1)} reshape(bf16[1,4,8,128,256]{3,2,4,1,0:T(8,128)(2,1)} %get-tuple-element.19) | data formatting | bytes 4194304 | tf_op jit(solution)/shard_map/while/body/eval_jaxpr/squeeze | solution.py:85
  64.8 2.9 %fusion = (f32[4,4,128]{2,1,0:T(4,128)S(1)}, f32[4,4,128,1024]{3,2,1,0:T(8,128)S(1)}) fusion(pred[4,1024]{1,0:T(4,128)(4,1)S(1)} %broadcast_compare_fusion, bf16[4,1024,4,64]{1,3,2,0:T(8,128)(2,1)} %squeeze.21, bf16[4,128,4,64]{3,2,1,0:T(4,128)(2,1)S(1)} %reshape.297), kind=kOutput, calls=%fused_computation.5 | convolution fusion | flops 274724864 | bytes 10760192 | tf_op jit(solution)/shard_map/while/body/eval_jaxpr/gqhd,gkhd->ghqk/dot_general | solution.py:84
  67.8 2.1 fusion.1
  69.9 2.2 fusion.34
  72.3 1.5 convolution_convert_fusion.1
  73.9 27.8 %reduce-scatter.2.cloned.1.call-done = bf16[512,256]{1,0:T(8,128)(2,1)} async-done(((bf16[512,1024]{1,0:T(8,128)(2,1)}), bf16[512,256]{1,0:T(8,128)(2,1)}) %reduce-scatter.2.cloned.1.call-update) | async-done | bytes 262160 | tf_op jit(solution)/shard_map/reduce_scatter | solution.py:221
  101.6 1.7 add_convert_fusion.1
  103.4 28.0 %all-gather.6.cloned.1.call-done = bf16[512,1024]{1,0:T(8,128)(2,1)} async-done(((bf16[512,256]{1,0:T(8,128)(2,1)}), bf16[512,1024]{1,0:T(8,128)(2,1)}) %all-gather.6.cloned.1.call-update) | async-done | bytes 1048592 | tf_op jit(solution)/shard_map/all_gather | solution.py:156
  131.4 1.5 fusion.6
  132.9 2.4 fusion.14
  135.4 0.8 convert_reduce_fusion.1
  136.2 0.9 fusion.56
  137.2 20.2 %all_to_all.16 = s32[64,1,4]{2,1,0:T(1,128)S(1)} all-to-all(s32[64,1,4]{2,1,0:T(1,128)S(1)} %broadcast_in_dim.100), channel_id=1, replica_groups=mesh['nodes'=64,'heads'=4] {'nodes'}, dimensions={0} | all-to-all | bytes 2048 | tf_op jit(solution)/shard_map/all_to_all | solution.py:31
  158.0 0.8 reduce.6
  159.4 48.5 %all-gather.2 = f32[64,4,128]{2,1,0:T(4,128)S(1)} all-gather(f32[1,4,128]{2,1,0:T(4,128)S(1)} %bitcast.138), channel_id=3, replica_groups=mesh['nodes'=64,'heads'=4] {'nodes'}, dimensions={0}, use_global_device_ids=true | all-gather | bytes 133120 | tf_op jit(solution)/shard_map/all_gather | solution.py:19
  208.0 0.7 fusion.27
  209.3 13.4 %all-gather.8.cloned.1.call-done = f32[256,128,64]{1,2,0:T(8,128)} async-done(((f32[4,128,64]{1,2,0:T(8,128)}), f32[256,128,64]{1,2,0:T(8,128)}) %all-gather.8.cloned.1.call-update) | async-done | bytes 8388624 | tf_op jit(solution)/shard_map/all_gather | solution.py:19
  222.7 3.9 %reduce_sum.116 = f32[4,128,64]{1,2,0:T(8,128)S(1)} reduce(f32[64,4,128,64]{2,3,1,0:T(8,128)} %bitcast.124, f32[]{:T(128)} %constant.91.clone.1), dimensions={0}, to_apply=%region_5.6 | reduce | flops 2064384 | bytes 8519684 | tf_op jit(solution)/shard_map/reduce_sum | solution.py:20
  226.6 0.7 fusion.19
  228.0 1.1 copy.62
  229.1 4.2 %all-to-all-start.1 = ((bf16[4,512,256]{2,1,0:T(8,128)(2,1)}), bf16[4,512,256]{2,1,0:T(8,128)(2,1)S(1)}, u32[]{:S(2)}, u32[]{:S(2)}) async-start(bf16[4,512,256]{2,1,0:T(8,128)(2,1)} %bitcast.126), calls=%async_computation.2 | async-start | bytes 2097152 | tf_op jit(solution)/shard_map/all_to_all | solution.py:59
  233.3 0.6 fusion.54
  233.9 1.8 collective-permute-start.7
  235.8 3.3 %collective-permute-start.6 = (s32[1,1]{1,0:T(1,128)}, s32[1,1]{1,0:T(1,128)}, u32[]{:S(2)}, u32[]{:S(2)}) collective-permute-start(s32[1,1]{1,0:T(1,128)} %get-tuple-element.41), channel_id=1, source_target_pairs={{0,128},{4,132},{8,136},{12,140},{16,144},{20,148},{24,152},{28,15... | collective-permute-start | bytes 20 | tf_op jit(solution)/shard_map/ppermute | solution.py:15
  239.1 3.2 %collective-permute-done.6 = s32[1,1]{1,0:T(1,128)} collective-permute-done((s32[1,1]{1,0:T(1,128)}, s32[1,1]{1,0:T(1,128)}, u32[]{:S(2)}, u32[]{:S(2)}) %collective-permute-start.6) | collective-permute-done | bytes 36 | tf_op jit(solution)/shard_map/ppermute | solution.py:15
  242.3 1.7 collective-permute-done.5
  243.9 2.6 add_subtract_fusion
  246.7 1.2 all-to-all-done.1
  248.7 1.9 collective-permute-start.4
  250.7 3.3 %collective-permute-start.3 = (bf16[1,1,128,256]{3,2,1,0:T(8,128)(2,1)S(1)}, bf16[1,1,128,256]{3,2,1,0:T(8,128)(2,1)S(1)}, u32[]{:S(2)}, u32[]{:S(2)}) collective-permute-start(bf16[1,1,128,256]{3,2,1,0:T(8,128)(2,1)S(1)} %get-tuple-element.37), channel_id=1, source_target_pairs={{0,128},{4,132},{8,136},{12,140},{16,144},{20,148},{24,152},{28,15... | collective-permute-start | bytes 196616 | tf_op jit(solution)/shard_map/ppermute | solution.py:15
  254.0 4.9 %collective-permute-done.3 = bf16[1,1,128,256]{3,2,1,0:T(8,128)(2,1)S(1)} collective-permute-done((bf16[1,1,128,256]{3,2,1,0:T(8,128)(2,1)S(1)}, bf16[1,1,128,256]{3,2,1,0:T(8,128)(2,1)S(1)}, u32[]{:S(2)}, u32[]{:S(2)}) %collective-permute-start.3) | collective-permute-done | bytes 65568 | tf_op jit(solution)/shard_map/ppermute | solution.py:15
  258.9 3.4 %collective-permute-done.2 = bf16[1,1,128,256]{3,2,1,0:T(8,128)(2,1)S(1)} collective-permute-done((bf16[1,1,128,256]{3,2,1,0:T(8,128)(2,1)S(1)}, bf16[1,1,128,256]{3,2,1,0:T(8,128)(2,1)S(1)}, u32[]{:S(2)}, u32[]{:S(2)}) %collective-permute-start.2) | collective-permute-done | bytes 65568 | tf_op jit(solution)/shard_map/ppermute | solution.py:15
  262.3 1.3 gather_fusion.2
  (74 shorter events, 5.2 us)
Async XLA Ops:
  6.5 22.8 %copy-start = (bf16[3,1024,256]{2,1,0:T(8,128)(2,1)S(1)}, bf16[3,1024,256]{2,1,0:T(8,128)(2,1)}, u32[]{:S(2)}) copy-start(bf16[3,1024,256]{2,1,0:T(8,128)(2,1)} %param.14) | copy-start | bytes 4718596
  6.5 6.5 %copy-start.7 = (s32[4,8]{1,0:T(4,128)S(1)}, s32[4,8]{1,0:T(4,128)}, u32[]{:S(2)}) copy-start(s32[4,8]{1,0:T(4,128)} %param.21) | copy-start | bytes 388
  8.7 18.6 %all-to-all-start = ((bf16[4,512,256]{2,1,0:T(8,128)(2,1)}), bf16[4,512,256]{2,1,0:T(8,128)(2,1)}, u32[]{:S(2)}, u32[]{:S(2)}) async-start(bf16[4,512,256]{2,1,0:T(8,128)(2,1)} %broadcast_in_dim.96), calls=%async_computation | async-start | bytes 2097152 | tf_op jit(solution)/shard_map/all_to_all | solution.py:31
  13.0 16.1 %copy-start.6 = (f32[1024]{0:T(1024)S(1)}, f32[1024]{0:T(1024)}, u32[]{:S(2)}) copy-start(f32[1024]{0:T(1024)} %param.13) | copy-start | bytes 12292
  13.0 88.7 %reduce-scatter.2.cloned.1.call-start = ((), (), s32[]{:S(2)}) async-start(), calls=%async_computation.4 | async-start | bytes 1310720 | tf_op jit(solution)/shard_map/reduce_scatter | solution.py:221
  29.4 7.9 %copy-start.9 = (s32[4]{0:T(128)S(1)}, s32[4]{0:T(128)}, u32[]{:S(2)}) copy-start(s32[4]{0:T(128)} %param.20) | copy-start | bytes 52
  30.5 8.9 %collective-permute-start.1 = (bf16[2,256,256]{2,1,0:T(8,128)(2,1)S(1)}, bf16[2,256,256]{2,1,0:T(8,128)(2,1)S(1)}, u32[]{:S(2)}, u32[]{:S(2)}) collective-permute-start(bf16[2,256,256]{2,1,0:T(8,128)(2,1)S(1)} %get-tuple-element.34), channel_id=1, source_target_pairs={{4,0},{8,4},{12,8},{16,12},{20,16},{24,20},{28,24},{32,28},{36,32}... | collective-permute-start | bytes 786440 | tf_op jit(solution)/shard_map/ppermute | solution.py:46
  34.2 6.3 %collective-permute-start = (bf16[2,256,256]{2,1,0:T(8,128)(2,1)S(1)}, bf16[2,256,256]{2,1,0:T(8,128)(2,1)}, u32[]{:S(2)}, u32[]{:S(2)}) collective-permute-start(bf16[2,256,256]{2,1,0:T(8,128)(2,1)S(1)} %get-tuple-element.33), channel_id=1, source_target_pairs={{0,4},{4,8},{8,12},{12,16},{16,20},{20,24},{24,28},{28,32},{32,36}... | collective-permute-start | bytes 786440 | tf_op jit(solution)/shard_map/ppermute | solution.py:45
  67.8 2.1 copy-start.2
  69.8 2.5 copy-start.4
  72.1 29.6 %copy-start.3 = (bf16[512,256]{1,0:T(8,128)(2,1)S(1)}, bf16[512,256]{1,0:T(8,128)(2,1)}, u32[]{:S(2)}) copy-start(bf16[512,256]{1,0:T(8,128)(2,1)} %param.12) | copy-start | bytes 786436
  72.3 60.6 %copy-start.11 = (bf16[3,1024,256]{2,1,0:T(8,128)(2,1)S(1)}, bf16[3,1024,256]{2,1,0:T(8,128)(2,1)}, u32[]{:S(2)}) copy-start(bf16[3,1024,256]{2,1,0:T(8,128)(2,1)} %param.17) | copy-start | bytes 4718596
  72.3 60.6 %copy-start.13 = (f32[1024]{0:T(1024)S(1)}, f32[1024]{0:T(1024)}, u32[]{:S(2)}) copy-start(f32[1024]{0:T(1024)} %param.16) | copy-start | bytes 12292
  73.8 57.6 %all-gather.6.cloned.1.call-start = ((), (), s32[]{:S(2)}) async-start(), calls=%async_computation.5 | async-start | bytes 1310720 | tf_op jit(solution)/shard_map/all_gather | solution.py:156
  103.4 119.3 %all-gather.8.cloned.1.call-start = ((), (), s32[]{:S(2)}) async-start(), calls=%async_computation.6 | async-start | bytes 8519680 | tf_op jit(solution)/shard_map/all_gather | solution.py:19
  132.9 2.5 copy-start.12
  135.4 1.7 copy-start.8
  135.4 23.4 %copy-start.10 = (s32[4]{0:T(128)S(1)}, s32[4]{0:T(128)}, u32[]{:S(2)}) copy-start(s32[4]{0:T(128)} %param.22) | copy-start | bytes 52
  226.5 1.0 copy-start.5
  229.1 19.0 %copy-start.1 = (bf16[512,256]{1,0:T(8,128)(2,1)S(1)}, bf16[512,256]{1,0:T(8,128)(2,1)}, u32[]{:S(2)}) copy-start(bf16[512,256]{1,0:T(8,128)(2,1)} %add_convert_fusion.1) | copy-start | bytes 786436
  229.1 18.8 %all-to-all-start.1 = ((bf16[4,512,256]{2,1,0:T(8,128)(2,1)}), bf16[4,512,256]{2,1,0:T(8,128)(2,1)S(1)}, u32[]{:S(2)}, u32[]{:S(2)}) async-start(bf16[4,512,256]{2,1,0:T(8,128)(2,1)} %bitcast.126), calls=%async_computation.2 | async-start | bytes 2097152 | tf_op jit(solution)/shard_map/all_to_all | solution.py:59
  233.9 5.2 %collective-permute-start.7 = (s32[1,1]{1,0:T(1,128)}, s32[1,1]{1,0:T(1,128)}, u32[]{:S(2)}, u32[]{:S(2)}) collective-permute-start(s32[1,1]{1,0:T(1,128)} %get-tuple-element.40), channel_id=1, source_target_pairs={{0,192},{4,196},{8,200},{12,204},{16,208},{20,212},{24,216},{28,22... | collective-permute-start | bytes 20 | tf_op jit(solution)/shard_map/ppermute | solution.py:15
  235.8 6.5 %collective-permute-start.6 = (s32[1,1]{1,0:T(1,128)}, s32[1,1]{1,0:T(1,128)}, u32[]{:S(2)}, u32[]{:S(2)}) collective-permute-start(s32[1,1]{1,0:T(1,128)} %get-tuple-element.41), channel_id=1, source_target_pairs={{0,128},{4,132},{8,136},{12,140},{16,144},{20,148},{24,152},{28,15... | collective-permute-start | bytes 20 | tf_op jit(solution)/shard_map/ppermute | solution.py:15
  239.1 4.8 %collective-permute-start.5 = (s32[1,1]{1,0:T(1,128)}, s32[1,1]{1,0:T(1,128)}, u32[]{:S(2)}, u32[]{:S(2)}) collective-permute-start(s32[1,1]{1,0:T(1,128)} %get-tuple-element.42), channel_id=1, source_target_pairs={{0,64},{4,68},{8,72},{12,76},{16,80},{20,84},{24,88},{28,92},{32,9... | collective-permute-start | bytes 20 | tf_op jit(solution)/shard_map/ppermute | solution.py:15
  248.7 5.2 %collective-permute-start.4 = (bf16[1,1,128,256]{3,2,1,0:T(8,128)(2,1)S(1)}, bf16[1,1,128,256]{3,2,1,0:T(8,128)(2,1)S(1)}, u32[]{:S(2)}, u32[]{:S(2)}) collective-permute-start(bf16[1,1,128,256]{3,2,1,0:T(8,128)(2,1)S(1)} %get-tuple-element.36), channel_id=1, source_target_pairs={{0,192},{4,196},{8,200},{12,204},{16,208},{20,212},{24,216},{28,22... | collective-permute-start | bytes 196616 | tf_op jit(solution)/shard_map/ppermute | solution.py:15
  250.7 8.2 %collective-permute-start.3 = (bf16[1,1,128,256]{3,2,1,0:T(8,128)(2,1)S(1)}, bf16[1,1,128,256]{3,2,1,0:T(8,128)(2,1)S(1)}, u32[]{:S(2)}, u32[]{:S(2)}) collective-permute-start(bf16[1,1,128,256]{3,2,1,0:T(8,128)(2,1)S(1)} %get-tuple-element.37), channel_id=1, source_target_pairs={{0,128},{4,132},{8,136},{12,140},{16,144},{20,148},{24,152},{28,15... | collective-permute-start | bytes 196616 | tf_op jit(solution)/shard_map/ppermute | solution.py:15
  254.0 8.3 %collective-permute-start.2 = (bf16[1,1,128,256]{3,2,1,0:T(8,128)(2,1)S(1)}, bf16[1,1,128,256]{3,2,1,0:T(8,128)(2,1)S(1)}, u32[]{:S(2)}, u32[]{:S(2)}) collective-permute-start(bf16[1,1,128,256]{3,2,1,0:T(8,128)(2,1)S(1)} %get-tuple-element.38), channel_id=1, source_target_pairs={{0,64},{4,68},{8,72},{12,76},{16,80},{20,84},{24,88},{28,92},{32,9... | collective-permute-start | bytes 196616 | tf_op jit(solution)/shard_map/ppermute | solution.py:15
Sparse Core Ops, SparseCore 0:
  73.9 27.6 reduce-scatter.1
  103.5 27.8 all-gather.5
  137.2 85.3 all-gather.7
where the time goes:
time: 271 us; the launch traced here: 270 us
  waiting for transfers between devices  99.8 us (37%)
  blocking collectives  68.7 us (25%)
  local copies, waits for them, and re-layouts  33 us (12%)
  starting transfers between devices  25.6 us (9%)
  other arithmetic  15.4 us (6%)
  matrix products  14 us (5%)
  between operations  13.5 us (5%)
    all_gather x1, blocking collectives, gathered_total(): parts = lax.all_gather(array, axis)  48.5 us
    all_gather x1, waiting for transfers between devices, gather_rows(): return lax.all_gather(shard_rows, 'heads', axis=1, tiled=True)  28 us
    reduce_scatter x1, waiting for transfers between devices, body(): lax.psum_scatter(partial_value.astype(jnp.bfloat16), 'heads', scatter_dim...  27.8 us
    all_to_all x1, blocking collectives, copy_for_each(): return lax.all_to_all(copies, axis, split_axis=0, concat_axis=0, tiled=True)  20.2 us
    all_to_all x1, waiting for transfers between devices, copy_for_each(): return lax.all_to_all(copies, axis, split_axis=0, concat_axis=0, tiled=True)  14.1 us
    all_gather x1, waiting for transfers between devices, gathered_total(): parts = lax.all_gather(array, axis)  13.4 us
    ppermute x6, waiting for transfers between devices, passed_along(): return lax.ppermute(value, axis, pairs)  13.1 us
    ppermute x6, starting transfers between devices, passed_along(): return lax.ppermute(value, axis, pairs)  10.4 us
  transfers between devices with their start and end apart: 13, of which 11 were waited for; matrix products, arithmetic and copies ran while one was open for 3% of the time, Pallas kernels for 0%

commit v1 on v0

--- a/solution.py
+++ b/solution.py
@@ -7,6 +7,11 @@
 BLOCK = 128
 HALO_BLK = 2
 EPSILON = 1e-06
+
+
+def gather_from_all(x, axis, dim):
+    copies = jnp.concatenate([x] * lax.axis_size(axis), axis=dim)
+    return lax.all_to_all(copies, axis, dim, dim, tiled=True)
 
 
 def passed_along(value, axis, steps):
@@ -153,7 +158,7 @@
 
 
 def gather_rows(shard_rows):
-    return lax.all_gather(shard_rows, "heads", axis=1, tiled=True)
+    return gather_from_all(shard_rows, "heads", 1)
 
 
 def global_mixing(full_rows, gain_vector, triple_weight, feature_map, out_weight):

time: 271 us -> 258 us (0.952)
  waiting for transfers between devices: 99.8 us -> 70.6 us
  blocking collectives: 68.7 us -> 86 us
    all_gather x1 -> x0, waiting for transfers between devices: 28 us -> none  [gather_rows(): return lax.all_gather(shard_rows, 'heads', axis=1, tiled=True)]
    all_to_all x0 -> x1, blocking collectives: none -> 15.8 us  [gather_from_all(): return lax.all_to_all(copies, axis, dim, dim, tiled=True)]
  transfers between devices with their start and end apart: 13 -> 12, of which waited for: 11 -> 10; matrix products, arithmetic and copies ran while one was open for 3% -> 3% of each run, Pallas kernels for 0% -> 0%
where the time goes in v1:
time: 258 us
  blocking collectives  86 us (33%)
  waiting for transfers between devices  70.6 us (27%)
  local copies, waits for them, and re-layouts  35.3 us (14%)
  starting transfers between devices  25.5 us (10%)
  between operations  13.8 us (5%)
  other arithmetic  13.7 us (5%)
  matrix products  12.7 us (5%)
    all_gather x1, blocking collectives, gathered_total(): parts = lax.all_gather(array, axis)  48.5 us
    reduce_scatter x1, waiting for transfers between devices, body(): lax.psum_scatter(partial_value.astype(jnp.bfloat16), 'heads', scatter_dim...  27.8 us
    all_to_all x1, blocking collectives, copy_for_each(): return lax.all_to_all(copies, axis, split_axis=0, concat_axis=0, tiled=True)  21.6 us
    all_to_all x1, blocking collectives, gather_from_all(): return lax.all_to_all(copies, axis, dim, dim, tiled=True)  15.8 us
    all_to_all x1, waiting for transfers between devices, copy_for_each(): return lax.all_to_all(copies, axis, split_axis=0, concat_axis=0, tiled=True)  14.1 us
    ppermute x6, waiting for transfers between devices, passed_along(): return lax.ppermute(value, axis, pairs)  13.1 us
    all_gather x1, waiting for transfers between devices, gathered_total(): parts = lax.all_gather(array, axis)  12 us
    ppermute x6, starting transfers between devices, passed_along(): return lax.ppermute(value, axis, pairs)  10.4 us
  transfers between devices with their start and end apart: 12, of which 10 were waited for; matrix products, arithmetic and copies ran while one was open for 3% of the time, Pallas kernels for 0%

profile of v1, /device:TPU:33, one launch (start us, length us, event | category | flops | bytes accessed | tf_op | source)
XLA Modules:
  0.0 257.5 jit_solution(7947857385784922037)
XLA Ops:
  6.5 2.2 broadcast_in_dim.96
  8.7 4.2 %all-to-all-start = ((bf16[4,512,256]{2,1,0:T(8,128)(2,1)}), bf16[4,512,256]{2,1,0:T(8,128)(2,1)}, u32[]{:S(2)}, u32[]{:S(2)}) async-start(bf16[4,512,256]{2,1,0:T(8,128)(2,1)} %broadcast_in_dim.96), calls=%async_computation | async-start | bytes 2097152 | tf_op jit(solution)/shard_map/all_to_all | solution.py:36
  13.1 14.1 %all-to-all-done = bf16[4,512,256]{2,1,0:T(8,128)(2,1)} async-done(((bf16[4,512,256]{2,1,0:T(8,128)(2,1)}), bf16[4,512,256]{2,1,0:T(8,128)(2,1)}, u32[]{:S(2)}, u32[]{:S(2)}) %all-to-all-start) | async-done | bytes 1048608 | tf_op jit(solution)/shard_map/all_to_all | solution.py:36
  27.3 1.5 copy.39
  29.4 1.0 fusion.12
  30.5 3.7 %collective-permute-start.1 = (bf16[2,256,256]{2,1,0:T(8,128)(2,1)S(1)}, bf16[2,256,256]{2,1,0:T(8,128)(2,1)S(1)}, u32[]{:S(2)}, u32[]{:S(2)}) collective-permute-start(bf16[2,256,256]{2,1,0:T(8,128)(2,1)S(1)} %get-tuple-element.34), channel_id=1, source_target_pairs={{4,0},{8,4},{12,8},{16,12},{20,16},{24,20},{28,24},{32,28},{36,32}... | collective-permute-start | bytes 786440 | tf_op jit(solution)/shard_map/ppermute | solution.py:51
  34.2 3.0 %collective-permute-start = (bf16[2,256,256]{2,1,0:T(8,128)(2,1)S(1)}, bf16[2,256,256]{2,1,0:T(8,128)(2,1)}, u32[]{:S(2)}, u32[]{:S(2)}) collective-permute-start(bf16[2,256,256]{2,1,0:T(8,128)(2,1)S(1)} %get-tuple-element.33), channel_id=1, source_target_pairs={{0,4},{4,8},{8,12},{12,16},{16,20},{20,24},{24,28},{28,32},{32,36}... | collective-permute-start | bytes 786440 | tf_op jit(solution)/shard_map/ppermute | solution.py:50
  37.3 0.8 slice.81
  38.4 0.9 collective-permute-done.1
  39.3 1.2 collective-permute-done
  40.5 1.2 pad_maximum_fusion
  41.7 2.8 %gather_fusion = bf16[32,2,128,256]{3,2,1,0:T(8,128)(2,1)} fusion(bf16[2,8,128,256]{3,2,1,0:T(8,128)(2,1)S(1)} %bitcast.131, s32[1024]{0:T(1024)S(1)} %pad_clamp_fusion.2), kind=kCustom, calls=%fused_computation | custom fusion | bytes 8388736 | tf_op jit(solution)/shard_map/while/body/eval_jaxpr/gather | solution.py:86
  44.5 7.5 %copy.41 = bf16[4,8,2,128,256]{3,1,4,0,2:T(8,128)(2,1)} copy(bf16[4,8,2,128,256]{4,3,2,1,0:T(8,128)(2,1)} %bitcast.132) | data formatting | bytes 8388608 | tf_op jit(solution)/shard_map/while/body/eval_jaxpr/gather | solution.py:86
  52.0 4.5 %fusion.46 = (bf16[1,4,8,128,256]{3,2,4,1,0:T(8,128)(2,1)}, bf16[1,4,8,128,256]{3,2,4,1,0:T(8,128)(2,1)}) fusion(bf16[2,4,8,128,256]{3,2,4,1,0:T(8,128)(2,1)} %bitcast.133), kind=kLoop, calls=%fused_computation.103 | loop fusion | bytes 8388608 | tf_op jit(solution)/shard_map/while/body/eval_jaxpr/slice | solution.py:90
  56.5 4.2 %squeeze.19 = bf16[4,1024,4,64]{1,3,2,0:T(8,128)(2,1)} reshape(bf16[1,4,8,128,256]{3,2,4,1,0:T(8,128)(2,1)} %get-tuple-element.20) | data formatting | bytes 4194304 | tf_op jit(solution)/shard_map/while/body/eval_jaxpr/squeeze | solution.py:99
  60.7 4.2 %squeeze.21 = bf16[4,1024,4,64]{1,3,2,0:T(8,128)(2,1)} reshape(bf16[1,4,8,128,256]{3,2,4,1,0:T(8,128)(2,1)} %get-tuple-element.19) | data formatting | bytes 4194304 | tf_op jit(solution)/shard_map/while/body/eval_jaxpr/squeeze | solution.py:90
  64.8 2.9 %fusion = (f32[4,4,128]{2,1,0:T(4,128)S(1)}, f32[4,4,128,1024]{3,2,1,0:T(8,128)S(1)}) fusion(pred[4,1024]{1,0:T(4,128)(4,1)S(1)} %broadcast_compare_fusion, bf16[4,1024,4,64]{1,3,2,0:T(8,128)(2,1)} %squeeze.21, bf16[4,128,4,64]{3,2,1,0:T(4,128)(2,1)S(1)} %reshape.302), kind=kOutput, calls=%fused_computation.5 | convolution fusion | flops 274724864 | bytes 10760192 | tf_op jit(solution)/shard_map/while/body/eval_jaxpr/gqhd,gkhd->ghqk/dot_general | solution.py:89
  67.8 2.1 fusion.1
  69.9 2.2 fusion.30
  72.3 1.5 convolution_convert_fusion.1
  73.9 27.8 %reduce-scatter.2.cloned.1.call-done = bf16[512,256]{1,0:T(8,128)(2,1)} async-done(((bf16[512,1024]{1,0:T(8,128)(2,1)}), bf16[512,256]{1,0:T(8,128)(2,1)}) %reduce-scatter.2.cloned.1.call-update) | async-done | bytes 262160 | tf_op jit(solution)/shard_map/reduce_scatter | solution.py:226
  101.6 1.0 add_convert_fusion.1
  102.8 15.8 %all_to_all.25 = bf16[512,4,256]{2,0,1:T(8,128)(2,1)} all-to-all(bf16[512,4,256]{2,0,1:T(8,128)(2,1)S(1)} %bitcast.138), channel_id=1, replica_groups=mesh['nodes'=64,'heads'=4] {'heads'}, dimensions={1} | all-to-all | bytes 2097152 | tf_op jit(solution)/shard_map/all_to_all | solution.py:14
  118.6 1.5 copy.46
  120.8 0.8 copy-done.11
  121.6 1.0 fusion.13
  122.7 0.8 convert_reduce_fusion.1
  123.5 0.9 fusion.52
  124.4 21.6 %all_to_all.26 = s32[64,1,4]{2,1,0:T(1,128)S(1)} all-to-all(s32[64,1,4]{2,1,0:T(1,128)S(1)} %broadcast_in_dim.100), channel_id=1, replica_groups=mesh['nodes'=64,'heads'=4] {'nodes'}, dimensions={0} | all-to-all | bytes 2048 | tf_op jit(solution)/shard_map/all_to_all | solution.py:36
  147.9 48.5 %all-gather.2 = f32[64,4,128]{2,1,0:T(4,128)S(1)} all-gather(f32[1,4,128]{2,1,0:T(4,128)S(1)} %bitcast.150), channel_id=3, replica_groups=mesh['nodes'=64,'heads'=4] {'nodes'}, dimensions={0}, use_global_device_ids=true | all-gather | bytes 133120 | tf_op jit(solution)/shard_map/all_gather | solution.py:24
  196.5 0.7 fusion.24
  197.7 12.0 %all-gather.5.cloned.1.call-done = f32[256,128,64]{1,2,0:T(8,128)} async-done(((f32[4,128,64]{1,2,0:T(8,128)}), f32[256,128,64]{1,2,0:T(8,128)}) %all-gather.5.cloned.1.call-update) | async-done | bytes 8388624 | tf_op jit(solution)/shard_map/all_gather | solution.py:24
  209.8 3.9 %reduce_sum.116 = f32[4,128,64]{1,2,0:T(8,128)S(1)} reduce(f32[64,4,128,64]{2,3,1,0:T(8,128)} %bitcast.134, f32[]{:T(128)} %constant.91.clone.1), dimensions={0}, to_apply=%region_5.6 | reduce | flops 2064384 | bytes 8519684 | tf_op jit(solution)/shard_map/reduce_sum | solution.py:25
  213.6 0.7 fusion.18
  215.1 1.1 copy.73
  216.2 4.0 %all-to-all-start.2 = ((bf16[4,512,256]{2,1,0:T(8,128)(2,1)}), bf16[4,512,256]{2,1,0:T(8,128)(2,1)S(1)}, u32[]{:S(2)}, u32[]{:S(2)}) async-start(bf16[4,512,256]{2,1,0:T(8,128)(2,1)} %bitcast.137), calls=%async_computation.3 | async-start | bytes 2097152 | tf_op jit(solution)/shard_map/all_to_all | solution.py:64
  220.2 0.7 fusion.50
  220.9 1.9 collective-permute-start.7
  222.7 3.3 %collective-permute-start.6 = (s32[1,1]{1,0:T(1,128)}, s32[1,1]{1,0:T(1,128)}, u32[]{:S(2)}, u32[]{:S(2)}) collective-permute-start(s32[1,1]{1,0:T(1,128)} %get-tuple-element.41), channel_id=1, source_target_pairs={{0,128},{4,132},{8,136},{12,140},{16,144},{20,148},{24,152},{28,15... | collective-permute-start | bytes 20 | tf_op jit(solution)/shard_map/ppermute | solution.py:20
  226.1 3.0 %collective-permute-done.6 = s32[1,1]{1,0:T(1,128)} collective-permute-done((s32[1,1]{1,0:T(1,128)}, s32[1,1]{1,0:T(1,128)}, u32[]{:S(2)}, u32[]{:S(2)}) %collective-permute-start.6) | collective-permute-done | bytes 36 | tf_op jit(solution)/shard_map/ppermute | solution.py:20
  229.1 1.7 collective-permute-done.5
  230.7 2.6 %add_subtract_fusion = s32[4]{0:T(128)S(1)} fusion(s32[1]{0:T(128)} %bitcast.35, s32[1]{0:T(128)} %bitcast.34, s32[1]{0:T(128)} %bitcast.33, s32[1]{0:T(128)} %bitcast.32, s32[]{:T(128)S(6)} %mul.73), kind=kLoop, calls=%fused_computation.99 | loop fusion | flops 16 | bytes 36 | tf_op jit(solution)/shard_map/sub | solution.py:152
  233.5 1.4 all-to-all-done.2
  235.7 1.9 collective-permute-start.4
  237.6 3.3 %collective-permute-start.3 = (bf16[1,1,128,256]{3,2,1,0:T(8,128)(2,1)S(1)}, bf16[1,1,128,256]{3,2,1,0:T(8,128)(2,1)S(1)}, u32[]{:S(2)}, u32[]{:S(2)}) collective-permute-start(bf16[1,1,128,256]{3,2,1,0:T(8,128)(2,1)S(1)} %get-tuple-element.37), channel_id=1, source_target_pairs={{0,128},{4,132},{8,136},{12,140},{16,144},{20,148},{24,152},{28,15... | collective-permute-start | bytes 196616 | tf_op jit(solution)/shard_map/ppermute | solution.py:20
  240.9 4.8 %collective-permute-done.3 = bf16[1,1,128,256]{3,2,1,0:T(8,128)(2,1)S(1)} collective-permute-done((bf16[1,1,128,256]{3,2,1,0:T(8,128)(2,1)S(1)}, bf16[1,1,128,256]{3,2,1,0:T(8,128)(2,1)S(1)}, u32[]{:S(2)}, u32[]{:S(2)}) %collective-permute-start.3) | collective-permute-done | bytes 65568 | tf_op jit(solution)/shard_map/ppermute | solution.py:20
  245.7 3.7 %collective-permute-done.2 = bf16[1,1,128,256]{3,2,1,0:T(8,128)(2,1)S(1)} collective-permute-done((bf16[1,1,128,256]{3,2,1,0:T(8,128)(2,1)S(1)}, bf16[1,1,128,256]{3,2,1,0:T(8,128)(2,1)S(1)}, u32[]{:S(2)}, u32[]{:S(2)}) %collective-permute-start.2) | collective-permute-done | bytes 65568 | tf_op jit(solution)/shard_map/ppermute | solution.py:20
  249.4 1.3 gather_fusion.2
  (74 shorter events, 6.4 us)
Async XLA Ops:
  6.5 22.8 %copy-start = (bf16[3,1024,256]{2,1,0:T(8,128)(2,1)S(1)}, bf16[3,1024,256]{2,1,0:T(8,128)(2,1)}, u32[]{:S(2)}) copy-start(bf16[3,1024,256]{2,1,0:T(8,128)(2,1)} %param.14) | copy-start | bytes 4718596
  6.5 6.5 %copy-start.7 = (s32[4,8]{1,0:T(4,128)S(1)}, s32[4,8]{1,0:T(4,128)}, u32[]{:S(2)}) copy-start(s32[4,8]{1,0:T(4,128)} %param.21) | copy-start | bytes 388
  8.7 18.6 %all-to-all-start = ((bf16[4,512,256]{2,1,0:T(8,128)(2,1)}), bf16[4,512,256]{2,1,0:T(8,128)(2,1)}, u32[]{:S(2)}, u32[]{:S(2)}) async-start(bf16[4,512,256]{2,1,0:T(8,128)(2,1)} %broadcast_in_dim.96), calls=%async_computation | async-start | bytes 2097152 | tf_op jit(solution)/shard_map/all_to_all | solution.py:36
  13.0 16.1 %copy-start.5 = (f32[1024]{0:T(1024)S(1)}, f32[1024]{0:T(1024)}, u32[]{:S(2)}) copy-start(f32[1024]{0:T(1024)} %param.13) | copy-start | bytes 12292
  13.0 88.6 %reduce-scatter.2.cloned.1.call-start = ((), (), s32[]{:S(2)}) async-start(), calls=%async_computation.5 | async-start | bytes 1310720 | tf_op jit(solution)/shard_map/reduce_scatter | solution.py:226
  29.4 7.9 %copy-start.9 = (s32[4]{0:T(128)S(1)}, s32[4]{0:T(128)}, u32[]{:S(2)}) copy-start(s32[4]{0:T(128)} %param.20) | copy-start | bytes 52
  30.5 8.9 %collective-permute-start.1 = (bf16[2,256,256]{2,1,0:T(8,128)(2,1)S(1)}, bf16[2,256,256]{2,1,0:T(8,128)(2,1)S(1)}, u32[]{:S(2)}, u32[]{:S(2)}) collective-permute-start(bf16[2,256,256]{2,1,0:T(8,128)(2,1)S(1)} %get-tuple-element.34), channel_id=1, source_target_pairs={{4,0},{8,4},{12,8},{16,12},{20,16},{24,20},{28,24},{32,28},{36,32}... | collective-permute-start | bytes 786440 | tf_op jit(solution)/shard_map/ppermute | solution.py:51
  34.2 6.3 %collective-permute-start = (bf16[2,256,256]{2,1,0:T(8,128)(2,1)S(1)}, bf16[2,256,256]{2,1,0:T(8,128)(2,1)}, u32[]{:S(2)}, u32[]{:S(2)}) collective-permute-start(bf16[2,256,256]{2,1,0:T(8,128)(2,1)S(1)} %get-tuple-element.33), channel_id=1, source_target_pairs={{0,4},{4,8},{8,12},{12,16},{16,20},{20,24},{24,28},{28,32},{32,36}... | collective-permute-start | bytes 786440 | tf_op jit(solution)/shard_map/ppermute | solution.py:50
  67.8 2.1 copy-start.1
  69.8 2.5 copy-start.3
  72.1 29.5 %copy-start.2 = (bf16[512,256]{1,0:T(8,128)(2,1)S(1)}, bf16[512,256]{1,0:T(8,128)(2,1)}, u32[]{:S(2)}) copy-start(bf16[512,256]{1,0:T(8,128)(2,1)} %param.12) | copy-start | bytes 786436
  73.8 135.9 %all-gather.5.cloned.1.call-start = ((), (), s32[]{:S(2)}) async-start(), calls=%async_computation.6 | async-start | bytes 8519680 | tf_op jit(solution)/shard_map/all_gather | solution.py:24
  118.6 1.8 copy-start.6
  120.1 1.4 copy-start.11
  121.6 1.1 copy-start.12
  122.6 1.7 copy-start.8
  122.7 24.7 %copy-start.10 = (s32[4]{0:T(128)S(1)}, s32[4]{0:T(128)}, u32[]{:S(2)}) copy-start(s32[4]{0:T(128)} %param.22) | copy-start | bytes 52
  213.6 1.0 copy-start.4
  216.2 18.7 %all-to-all-start.2 = ((bf16[4,512,256]{2,1,0:T(8,128)(2,1)}), bf16[4,512,256]{2,1,0:T(8,128)(2,1)S(1)}, u32[]{:S(2)}, u32[]{:S(2)}) async-start(bf16[4,512,256]{2,1,0:T(8,128)(2,1)} %bitcast.137), calls=%async_computation.3 | async-start | bytes 2097152 | tf_op jit(solution)/shard_map/all_to_all | solution.py:64
  220.9 5.2 %collective-permute-start.7 = (s32[1,1]{1,0:T(1,128)}, s32[1,1]{1,0:T(1,128)}, u32[]{:S(2)}, u32[]{:S(2)}) collective-permute-start(s32[1,1]{1,0:T(1,128)} %get-tuple-element.40), channel_id=1, source_target_pairs={{0,192},{4,196},{8,200},{12,204},{16,208},{20,212},{24,216},{28,22... | collective-permute-start | bytes 20 | tf_op jit(solution)/shard_map/ppermute | solution.py:20
  222.7 6.3 %collective-permute-start.6 = (s32[1,1]{1,0:T(1,128)}, s32[1,1]{1,0:T(1,128)}, u32[]{:S(2)}, u32[]{:S(2)}) collective-permute-start(s32[1,1]{1,0:T(1,128)} %get-tuple-element.41), channel_id=1, source_target_pairs={{0,128},{4,132},{8,136},{12,140},{16,144},{20,148},{24,152},{28,15... | collective-permute-start | bytes 20 | tf_op jit(solution)/shard_map/ppermute | solution.py:20
  226.0 4.7 %collective-permute-start.5 = (s32[1,1]{1,0:T(1,128)}, s32[1,1]{1,0:T(1,128)}, u32[]{:S(2)}, u32[]{:S(2)}) collective-permute-start(s32[1,1]{1,0:T(1,128)} %get-tuple-element.42), channel_id=1, source_target_pairs={{0,64},{4,68},{8,72},{12,76},{16,80},{20,84},{24,88},{28,92},{32,9... | collective-permute-start | bytes 20 | tf_op jit(solution)/shard_map/ppermute | solution.py:20
  235.7 5.3 %collective-permute-start.4 = (bf16[1,1,128,256]{3,2,1,0:T(8,128)(2,1)S(1)}, bf16[1,1,128,256]{3,2,1,0:T(8,128)(2,1)S(1)}, u32[]{:S(2)}, u32[]{:S(2)}) collective-permute-start(bf16[1,1,128,256]{3,2,1,0:T(8,128)(2,1)S(1)} %get-tuple-element.36), channel_id=1, source_target_pairs={{0,192},{4,196},{8,200},{12,204},{16,208},{20,212},{24,216},{28,22... | collective-permute-start | bytes 196616 | tf_op jit(solution)/shard_map/ppermute | solution.py:20
  237.6 8.1 %collective-permute-start.3 = (bf16[1,1,128,256]{3,2,1,0:T(8,128)(2,1)S(1)}, bf16[1,1,128,256]{3,2,1,0:T(8,128)(2,1)S(1)}, u32[]{:S(2)}, u32[]{:S(2)}) collective-permute-start(bf16[1,1,128,256]{3,2,1,0:T(8,128)(2,1)S(1)} %get-tuple-element.37), channel_id=1, source_target_pairs={{0,128},{4,132},{8,136},{12,140},{16,144},{20,148},{24,152},{28,15... | collective-permute-start | bytes 196616 | tf_op jit(solution)/shard_map/ppermute | solution.py:20
  240.9 8.5 %collective-permute-start.2 = (bf16[1,1,128,256]{3,2,1,0:T(8,128)(2,1)S(1)}, bf16[1,1,128,256]{3,2,1,0:T(8,128)(2,1)S(1)}, u32[]{:S(2)}, u32[]{:S(2)}) collective-permute-start(bf16[1,1,128,256]{3,2,1,0:T(8,128)(2,1)S(1)} %get-tuple-element.38), channel_id=1, source_target_pairs={{0,64},{4,68},{8,72},{12,76},{16,80},{20,84},{24,88},{28,92},{32,9... | collective-permute-start | bytes 196616 | tf_op jit(solution)/shard_map/ppermute | solution.py:20
Sparse Core Ops, SparseCore 0:
  73.9 27.6 reduce-scatter.1
  124.5 85.2 all-gather.4
